TPU v7x, 32 devices: a whole 2x2x4 slice. The times are simulated.
32 devices in a mesh: dp: 8 (over y, x, core), seq: 4 (over z).
Axes of the slice: x: 2, y: 2, z: 4, core: 2. Of those that a mesh axis runs over, the one named last changes fastest.
Arguments:
- tile_tokens: bfloat16 [8, 128, 3200], P('dp', 'seq'), may hold values from -6 to 6
- proj_weight: bfloat16 [3200, 8192], P('dp', 'seq')
- text_hidden: bfloat16 [8, 512, 8192], P('dp', 'seq'), may hold values from -6 to 6
- cotangent: bfloat16 [8, 512, 8192], P('dp', 'seq'), may hold values from -1.1953125 to 1.1953125
- norm_gain: float32 [8192], replicated, may hold values from 0.25 to 1.75
- placeholders: int32 [8, 128], P('dp'), may hold values from 0 to 511, as said below
- bucket_levels: int32 [8, 4, 3200], P('dp', 'seq'), may hold values from 2 to 16
- row_draws: float32 [8, 4, 3200], P('dp', 'seq'), may hold values from 0 to 1
- column_draws: float32 [8, 8192], P('dp', 'seq'), may hold values from 0 to 1
Outputs:
- weight_grad: float32 [3200, 8192], P('dp', 'seq')
- gain_grad: float32 [8192], replicated
Inputs may be any that keep to these rules, and one draw needn't show every extreme that they name: Each row is strictly increasing. Among the positions of one device's block of 128 positions stand at most 48 placeholders, and in every row some block holds exactly 48.
All inputs are finite; a program needn't handle non-finite values.
Results may differ from a plain program's by a relative error of at most 0.014.
Values may be sent and summed in bfloat16 or wider, within the bound.
No kernel may reach another device: no remote copies, remote signals or barrier semaphores. Data moves between devices by JAX's collectives and lax.ppermute only.
A program may use at most 64 MiB of HBM per device.

v0:
```python
import jax
import jax.numpy as jnp
from jax import lax
from jax.sharding import PartitionSpec as P

IMG_MOST = 48
EPSILON = 1e-06


def quantize(gradient, levels_now, rows_now, columns_now):
    bucket_norm = jnp.sqrt(jnp.sum(gradient * gradient, axis=1, keepdims=True) + EPSILON)
    step_count = levels_now.astype(jnp.float32)[:, None]
    offset = 0.25 + 0.25 * (rows_now[:, None] + columns_now[None, :])
    ratio = jnp.abs(gradient) / bucket_norm * step_count
    lower = jnp.floor(ratio)
    quantum = lower + jnp.clip(2.0 * (ratio - lower - offset) + 0.5, 0.0, 1.0)
    return jnp.sign(gradient) * bucket_norm * quantum / step_count


def on_device(
    tile_tokens,
    proj_weight,
    text_hidden,
    cotangent,
    norm_gain,
    placeholders,
    bucket_levels,
    row_draws,
    column_draws,
):
    seq_count = lax.axis_size("seq")
    seq_index = lax.axis_index("seq")
    replicas = lax.axis_size("dp")
    places = placeholders[0]
    image_total = places.shape[0]
    tok_rows = text_hidden.shape[1]
    model_width = text_hidden.shape[2]
    columns = proj_weight.shape[1]
    all_positions = tok_rows * seq_count
    zero_half = jnp.zeros((), jnp.bfloat16)
    own_text = text_hidden[0]
    own_cot = cotangent[0]
    gathered = lax.all_gather(tile_tokens[0], "seq", axis=0, tiled=True)
    patch_block = gathered
    embedded = jnp.dot(
        patch_block,
        lax.all_gather(proj_weight, "dp", axis=0, tiled=True),
        preferred_element_type=jnp.float32,
    ).astype(jnp.bfloat16)
    image_marks = jnp.zeros((all_positions,), jnp.int32).at[places].set(1)
    local_marks = lax.dynamic_slice_in_dim(image_marks, seq_index * tok_rows, tok_rows)
    is_image = local_marks[:, None] == 1
    owners = places // tok_rows
    owner_ids = jnp.arange(seq_count, dtype=jnp.int32)
    counts = jnp.sum((owners[:, None] == owner_ids[None, :]).astype(jnp.int32), axis=0)
    starts = jnp.cumsum(counts) - counts
    own_start = starts[seq_index]
    own_count = counts[seq_index]
    slot_ids = jnp.arange(IMG_MOST, dtype=jnp.int32)
    source_rows = jnp.clip(own_start + slot_ids, 0, image_total - 1)
    local_slots = jnp.clip(jnp.take(places, source_rows) - seq_index * tok_rows, 0, tok_rows - 1)
    slot_live = (slot_ids < own_count)[:, None]
    flat_index = owners * IMG_MOST + (
        jnp.arange(image_total, dtype=jnp.int32) - jnp.take(starts, owners)
    )
    outgoing = jnp.where(slot_live, jnp.take(own_cot, local_slots, axis=0), zero_half)
    returned = lax.all_to_all(outgoing[None], "seq", split_axis=2, concat_axis=0, tiled=True)
    image_cot = jnp.take(returned.reshape(-1, columns), flat_index, axis=0).astype(jnp.float32)
    emb_float = embedded.astype(jnp.float32)
    column_gain = lax.dynamic_slice_in_dim(norm_gain, seq_index * columns, columns)
    grad_in = image_cot * column_gain[None, :]
    squares, mixed = lax.psum(
        (jnp.sum(emb_float * emb_float, axis=1), jnp.sum(grad_in * emb_float, axis=1)), "seq"
    )
    inverse = lax.rsqrt(squares / model_width + EPSILON)[:, None]
    normed = emb_float * inverse
    emb_grad = ((grad_in - normed * (mixed[:, None] * inverse / model_width)) * inverse).astype(
        jnp.bfloat16
    )
    image_part = jnp.sum(image_cot * normed, axis=0)
    text_float = own_text.astype(jnp.float32)
    text_inverse = lax.rsqrt(jnp.mean(text_float * text_float, axis=1, keepdims=True) + EPSILON)
    text_terms = own_cot.astype(jnp.float32) * text_float * text_inverse
    text_part = jnp.sum(jnp.where(is_image, 0.0, text_terms), axis=0)
    placed_part = lax.dynamic_update_slice_in_dim(
        jnp.zeros((model_width,), jnp.float32), image_part, seq_index * columns, 0
    )
    gain_part = text_part + placed_part
    own_levels = bucket_levels[0, 0]
    own_row_draws = row_draws[0, 0]
    own_column_draws = column_draws[0]
    patch_block = gathered
    gradient = lax.dot_general(
        patch_block, emb_grad, (((0,), (0,)), ((), ())), preferred_element_type=jnp.float32
    )
    summed = lax.psum_scatter(
        quantize(gradient, own_levels, own_row_draws, own_column_draws).astype(jnp.bfloat16),
        "dp",
        scatter_dimension=0,
        tiled=True,
    ).astype(jnp.float32)
    gain_total = lax.psum(gain_part, ("dp", "seq"))
    return (summed / replicas, gain_total / replicas)


def solution(mesh):
    return jax.shard_map(
        on_device,
        mesh=mesh,
        in_specs=(
            P("dp", "seq", None),
            P("dp", "seq"),
            P("dp", "seq", None),
            P("dp", "seq", None),
            P(),
            P("dp", None),
            P("dp", "seq", None),
            P("dp", "seq", None),
            P("dp", "seq"),
        ),
        out_specs=(P("dp", "seq"), P()),
        check_vma=False,
    )
```

profile of v0, /device:TPU:0, one launch (start us, length us, event | category | flops | bytes accessed | tf_op | source)
XLA Modules:
  0.0 315.0 jit_solution(2458585537406789046)
XLA Ops:
  10.9 1.4 gather_fusion
  13.0 3.6 %gather_fusion.1 = bf16[48,8192]{1,0:T(8,128)(2,1)S(1)} fusion(bf16[128,8192]{1,0:T(8,128)(2,1)} %bitcast.74, s32[1024]{0:T(1024)S(1)} %pad_clamp_fusion.1), kind=kCustom, calls=%fused_computation.1 | custom fusion | bytes 1573056 | tf_op jit(solution)/shard_map/jit(_take)/gather | solution.py:66
  16.6 1.3 compare_and_fusion
  18.1 6.8 %copy.22 = bf16[1,48,8192]{1,0,2:T(2,128)(2,1)} copy(bf16[1,48,8192]{2,1,0:T(8,128)(2,1)S(1)} %fusion.21) | data formatting | bytes 1572864 | tf_op jit(solution)/shard_map/jit(_where)/select_n | solution.py:66
  25.3 45.2 %reduce.4 = bf16[8192,48]{1,0:T(8,128)(2,1)S(1)} reduce(bf16[8192,1,48]{2,1,0:T(2,128)(2,1)} %bitcast.76, bf16[]{:T(256)} %broadcast.575), dimensions={1}, to_apply=%bitcast.63.reduce_sub_computation | reduce | bytes 1572866
  70.6 4.0 %reshape.423 = bf16[4,2,49152]{2,1,0:T(2,128)(2,1)} reshape(bf16[8192,48]{1,0:T(8,128)(2,1)S(1)} %reduce.4) | data formatting | bytes 1572864
  74.6 6.3 %all-to-all-start = ((bf16[4,2,49152]{2,1,0:T(2,128)(2,1)}), bf16[4,2,49152]{2,1,0:T(2,128)(2,1)S(1)}, u32[]{:S(2)}, u32[]{:S(2)}) async-start(bf16[4,2,49152]{2,1,0:T(2,128)(2,1)} %reshape.423), calls=%async_computation | async-start | bytes 1572864 | tf_op jit(solution)/shard_map/all_to_all | solution.py:67
  81.7 2.6 compare_and_fusion.1
  84.4 30.7 %all-gather = bf16[1,128,3200]{2,1,0:T(8,128)(2,1)S(1)} all-gather(bf16[1,32,3200]{2,1,0:T(8,128)(2,1)S(1)} %copy-done.4), channel_id=2, replica_groups=mesh['dp'=8,'seq'=4] {'seq'}, dimensions={1}, use_global_device_ids=true | all-gather | bytes 1024000 | tf_op jit(solution)/shard_map/all_gather | solution.py:43
  115.0 4.6 %reshape.424 = bf16[8192,1,48]{2,1,0:T(2,128)(2,1)} reshape(bf16[4,2,49152]{2,1,0:T(2,128)(2,1)S(1)} %all-to-all-done) | data formatting | bytes 1572864
  119.6 8.1 %copy.23 = bf16[1,48,8192]{2,1,0:T(8,128)(2,1)S(1)} copy(bf16[1,48,8192]{1,0,2:T(2,128)(2,1)} %bitcast.77) | data formatting | bytes 1572864 | tf_op jit(solution)/shard_map/all_to_all | solution.py:67
  129.8 7.1 %multiply_reduce_fusion.1 = (f32[128]{0:T(128)S(1)}, f32[128,2048]{1,0:T(8,128)S(1)}) fusion(bf16[3200,2048]{1,0:T(8,128)(2,1)} %all-gather.3.cloned.1.call-done, bf16[1,128,3200]{2,1,0:T(8,128)(2,1)S(1)} %all-gather), kind=kOutput, calls=%fused_computation.31 | convolution fusion | flops 1678770048 | bytes 14975488 | tf_op jit(solution)/shard_map/dot_general | solution.py:45
  136.9 11.1 %psum.21 = f32[128]{0:T(128)S(1)} all-reduce(f32[128]{0:T(128)S(1)} %get-tuple-element.22), channel_id=1, replica_groups=mesh['dp'=8,'seq'=4] {'seq'}, use_global_device_ids=true, to_apply=%region_3.4 | all-reduce | flops 128 | bytes 1024 | tf_op jit(solution)/shard_map/psum | solution.py:72
  148.4 8.4 %psum.22 = f32[128]{0:T(128)S(1)} all-reduce(f32[128]{0:T(128)S(1)} %get-tuple-element.13), channel_id=1, replica_groups=mesh['dp'=8,'seq'=4] {'seq'}, use_global_device_ids=true, to_apply=%region_5.6 | all-reduce | flops 128 | bytes 1024 | tf_op jit(solution)/shard_map/psum | solution.py:72
  156.8 5.1 %multiply_reduce_fusion = (f32[3200]{0:T(1024)S(1)}, f32[2048,3200]{1,0:T(8,128)S(1)}) fusion(bf16[1,128,3200]{2,1,0:T(8,128)(2,1)S(1)} %all-gather, f32[128,2048]{1,0:T(8,128)} %copy-done.2, f32[128]{0:T(128)S(1)} %multiply_multiply_fusion, f32[128]{0:T(128)S(1)} %add_rsqrt_fusion.1, f32[2048]{0:T(1024)S(1)} %dynamic_slice.14, ...), kind=kOutput, calls=%fused_computation.12 | convolution fusion | flops 1692922752 | bytes 28628608 | tf_op jit(solution)/shard_map/dot_general | solution.py:93
  162.0 22.2 %fusion.6 = bf16[3200,2048]{0,1:T(8,128)(2,1)} fusion(f32[2048,3200]{1,0:T(8,128)S(1)} %get-tuple-element.25, f32[3200]{0:T(1024)S(1)} %convert_reduce_fusion, f32[2048]{0:T(1024)S(1)} %bitcast.79, f32[3200]{0:T(1024)S(1)} %reduce.2, f32[3200]{0:T(1024)S(1)} %add_sqrt_fusion), kind=kLoop, calls=%fused_computation.13 | loop fusion | flops 117964800 | bytes 39368192 | tf_op jit(solution)/shard_map/convert_element_type | solution.py:97
  184.1 18.3 %copy.26 = bf16[3200,2048]{1,0:T(8,128)(2,1)} copy(bf16[3200,2048]{0,1:T(8,128)(2,1)} %fusion.6) | data formatting | bytes 26214400
  203.6 2.1 fusion.10
  205.7 2.6 fusion.9
  208.3 41.3 %psum.23 = f32[8192]{0:T(1024)S(1)} all-reduce(f32[8192]{0:T(1024)S(1)} %add_dynamic-update-slice_fusion), channel_id=1, replica_groups=mesh['dp'=8,'seq'=4] {'dp','seq'}, use_global_device_ids=true, to_apply=%region_12.13 | all-reduce | flops 8192 | bytes 65536 | tf_op jit(solution)/shard_map/psum | solution.py:102
  250.3 47.4 %reduce-scatter.4.cloned.1.call-done = bf16[400,2048]{1,0:T(8,128)(2,1)} async-done(((bf16[3200,2048]{1,0:T(8,128)(2,1)}), bf16[400,2048]{1,0:T(8,128)(2,1)}) %reduce-scatter.4.cloned.1.call-update) | async-done | bytes 1638416
  297.7 2.8 copy.27
  300.5 2.5 convert_multiply_fusion.2
  303.0 5.2 %copy.25 = f32[400,2048]{1,0:T(8,128)} copy(f32[400,2048]{0,1:T(8,128)} %convert_multiply_fusion.2) | data formatting | bytes 6553600
  (53 shorter events, 10.0 us)
Async XLA Ops:
  7.2 74.5 %copy-start = (s32[1,128]{1,0:T(1,128)S(1)}, s32[1,128]{1,0:T(1,128)}, u32[]{:S(2)}) copy-start(s32[1,128]{1,0:T(1,128)} %param.14) | copy-start | bytes 1540
  7.2 74.5 %copy-start.6 = (f32[1,1,3200]{2,1,0:T(1,128)S(1)}, f32[1,1,3200]{2,1,0:T(1,128)}, u32[]{:S(2)}) copy-start(f32[1,1,3200]{2,1,0:T(1,128)} %param.16) | copy-start | bytes 38404
  7.2 77.1 %copy-start.5 = (s32[1,1,3200]{2,1,0:T(1,128)S(1)}, s32[1,1,3200]{2,1,0:T(1,128)}, u32[]{:S(2)}) copy-start(s32[1,1,3200]{2,1,0:T(1,128)} %param.15) | copy-start | bytes 38404
  7.2 77.2 %copy-start.4 = (bf16[1,32,3200]{2,1,0:T(8,128)(2,1)S(1)}, bf16[1,32,3200]{2,1,0:T(8,128)(2,1)}, u32[]{:S(2)}) copy-start(bf16[1,32,3200]{2,1,0:T(8,128)(2,1)} %param.9) | copy-start | bytes 614404
  7.2 122.6 %all-gather.3.cloned.1.call-start = ((), (), s32[]{:S(2)}) async-start(), calls=%async_computation.2 | async-start | bytes 14745600 | tf_op jit(solution)/shard_map/all_gather | solution.py:47
  74.6 40.5 %all-to-all-start = ((bf16[4,2,49152]{2,1,0:T(2,128)(2,1)}), bf16[4,2,49152]{2,1,0:T(2,128)(2,1)S(1)}, u32[]{:S(2)}, u32[]{:S(2)}) async-start(bf16[4,2,49152]{2,1,0:T(2,128)(2,1)} %reshape.423), calls=%async_computation | async-start | bytes 1572864 | tf_op jit(solution)/shard_map/all_to_all | solution.py:67
  80.9 216.8 %reduce-scatter.4.cloned.1.call-start = ((), (), s32[]{:S(2)}) async-start(), calls=%async_computation.3 | async-start | bytes 14745600
  129.7 27.0 %copy-start.3 = (bf16[128,2048]{1,0:T(8,128)(2,1)}, bf16[128,2048]{1,0:T(8,128)(2,1)S(1)}, u32[]{:S(2)}) copy-start(bf16[128,2048]{1,0:T(8,128)(2,1)S(1)} %gather_fusion.2) | copy-start | bytes 1572868
  136.8 19.9 %copy-start.2 = (f32[128,2048]{1,0:T(8,128)}, f32[128,2048]{1,0:T(8,128)S(1)}, u32[]{:S(2)}) copy-start(f32[128,2048]{1,0:T(8,128)S(1)} %get-tuple-element.23) | copy-start | bytes 3145732
  156.8 5.2 %copy-start.7 = (f32[1,2048]{1,0:T(1,128)S(1)}, f32[1,2048]{1,0:T(1,128)}, u32[]{:S(2)}) copy-start(f32[1,2048]{1,0:T(1,128)} %param.17) | copy-start | bytes 24580
  202.5 3.2 %copy-start.1 = (bf16[1,128,8192]{2,1,0:T(8,128)(2,1)S(1)}, bf16[1,128,8192]{2,1,0:T(8,128)(2,1)}, u32[]{:S(2)}) copy-start(bf16[1,128,8192]{2,1,0:T(8,128)(2,1)} %param.12) | copy-start | bytes 6291460
Sparse Core Ops, SparseCore 0:
  9.9 76.9 all-gather.2
  202.6 95.0 reduce-scatter.3
where the time goes:
time: 316 us; the launch traced here: 315 us
  blocking collectives  91.5 us (29%)
  other arithmetic  82.2 us (26%)
  local copies, waits for them, and re-layouts  60.3 us (19%)
  waiting for transfers between devices  48.1 us (15%)
  between operations  14.3 us (5%)
  matrix products  12.2 us (4%)
  starting transfers between devices  6.39 us (2%)
    unnamed x3, waiting for transfers between devices  48.1 us
    unnamed x2, other arithmetic  45.3 us
    psum x1, blocking collectives, on_device(): gain_total = lax.psum(gain_part, ('dp', 'seq'))  41.3 us
    unnamed x22, local copies, waits for them, and re-layouts  35.4 us
    all_gather x1, blocking collectives, on_device(): gathered = lax.all_gather(tile_tokens[0], 'seq', axis=0, tiled=True)  30.7 us
    convert_element_type x1, other arithmetic, on_device(): quantize(gradient, own_levels, own_row_draws, own_column_draws)  22.2 us
    psum x2, blocking collectives, on_device(): lax.psum((jnp.sum(emb_float * emb_float, axis=1), jnp.sum(grad_in * emb_f...  19.5 us
    all_to_all x3, local copies, waits for them, and re-layouts, on_device(): lax.all_to_all(outgoing[None], 'seq', split_axis=2, concat_axis=0, tiled=...  9.14 us
  transfers between devices with their start and end apart: 3, of which 1 were waited for; matrix products, arithmetic and copies ran while one was open for 29% of the time, Pallas kernels for 0%

commit v1 on v0

--- a/solution.py
+++ b/solution.py
@@ -99,7 +99,7 @@
         scatter_dimension=0,
         tiled=True,
     ).astype(jnp.float32)
-    gain_total = lax.psum(gain_part, ("dp", "seq"))
+    gain_total = lax.psum(lax.psum(gain_part, "seq"), "dp")
     return (summed / replicas, gain_total / replicas)
 
 

time: 316 us -> 333 us (1.054)
  waiting for transfers between devices: 48.1 us -> 71.9 us
  blocking collectives: 91.5 us -> 77.4 us
  local copies, waits for them, and re-layouts: 60.3 us -> 64.8 us
    unnamed x3, waiting for transfers between devices: 48.1 us -> 71.8 us
    psum x1, blocking collectives: 41.3 us -> 22.3 us  [on_device(): gain_total = lax.psum(lax.psum(gain_part, 'seq'), 'dp')]
    psum x2, blocking collectives: 19.5 us -> 27.6 us  [on_device(): lax.psum((jnp.sum(emb_float * emb_float, axis=1), jnp.sum(grad_in * emb_f...]
where the time goes in v1:
time: 333 us; the launch traced here: 331 us
  other arithmetic  84 us (25%)
  blocking collectives  77.4 us (23%)
  waiting for transfers between devices  71.9 us (22%)
  local copies, waits for them, and re-layouts  64.8 us (19%)
  between operations  14.3 us (4%)
  matrix products  12 us (4%)
  starting transfers between devices  6.49 us (2%)
    unnamed x3, waiting for transfers between devices  71.8 us
    unnamed x2, other arithmetic  46.5 us
    unnamed x22, local copies, waits for them, and re-layouts  37.7 us
    psum x2, blocking collectives, on_device(): lax.psum((jnp.sum(emb_float * emb_float, axis=1), jnp.sum(grad_in * emb_f...  27.6 us
    all_gather x1, blocking collectives, on_device(): gathered = lax.all_gather(tile_tokens[0], 'seq', axis=0, tiled=True)  27.5 us
    psum x1, blocking collectives, on_device(): gain_total = lax.psum(lax.psum(gain_part, 'seq'), 'dp')  22.3 us
    convert_element_type x1, other arithmetic, on_device(): quantize(gradient, own_levels, own_row_draws, own_column_draws)  22.1 us
    all_to_all x3, local copies, waits for them, and re-layouts, on_device(): lax.all_to_all(outgoing[None], 'seq', split_axis=2, concat_axis=0, tiled=...  9.14 us
  transfers between devices with their start and end apart: 3, of which 1 were waited for; matrix products, arithmetic and copies ran while one was open for 29% of the time, Pallas kernels for 0%

profile of v1, /device:TPU:0, one launch (start us, length us, event | category | flops | bytes accessed | tf_op | source)
XLA Modules:
  0.0 330.9 jit_solution(4915978098089223868)
XLA Ops:
  10.8 1.4 gather_fusion
  13.0 3.8 %gather_fusion.1 = bf16[48,8192]{1,0:T(8,128)(2,1)S(1)} fusion(bf16[128,8192]{1,0:T(8,128)(2,1)} %bitcast.75, s32[1024]{0:T(1024)S(1)} %pad_clamp_fusion.1), kind=kCustom, calls=%fused_computation.1 | custom fusion | bytes 1573056 | tf_op jit(solution)/shard_map/jit(_take)/gather | solution.py:66
  16.8 1.3 compare_and_fusion
  19.1 8.9 %copy.22 = bf16[1,48,8192]{1,0,2:T(2,128)(2,1)} copy(bf16[1,48,8192]{2,1,0:T(8,128)(2,1)} %fusion.21) | data formatting | bytes 1572864 | tf_op jit(solution)/shard_map/jit(_where)/select_n | solution.py:66
  28.5 46.5 %reduce.4 = bf16[8192,48]{1,0:T(8,128)(2,1)} reduce(bf16[8192,1,48]{2,1,0:T(2,128)(2,1)} %bitcast.77, bf16[]{:T(256)} %broadcast.575), dimensions={1}, to_apply=%bitcast.63.reduce_sub_computation | reduce | bytes 1572866
  74.9 5.1 %reshape.423 = bf16[4,2,49152]{2,1,0:T(2,128)(2,1)} reshape(bf16[8192,48]{1,0:T(8,128)(2,1)} %reduce.4) | data formatting | bytes 1572864
  80.0 6.5 %all-to-all-start = ((bf16[4,2,49152]{2,1,0:T(2,128)(2,1)}), bf16[4,2,49152]{2,1,0:T(2,128)(2,1)}, u32[]{:S(2)}, u32[]{:S(2)}) async-start(bf16[4,2,49152]{2,1,0:T(2,128)(2,1)} %reshape.423), calls=%async_computation | async-start | bytes 1572864 | tf_op jit(solution)/shard_map/all_to_all | solution.py:67
  87.5 2.5 compare_and_fusion.1
  90.9 2.1 fusion.10
  93.0 27.5 %all-gather = bf16[1,128,3200]{2,1,0:T(8,128)(2,1)S(1)} all-gather(bf16[1,32,3200]{2,1,0:T(8,128)(2,1)S(1)} %copy-done.4), channel_id=2, replica_groups=mesh['dp'=8,'seq'=4] {'seq'}, dimensions={1}, use_global_device_ids=true | all-gather | bytes 1024000 | tf_op jit(solution)/shard_map/all_gather | solution.py:43
  120.5 2.5 fusion.9
  123.0 5.8 %reshape.424 = bf16[8192,1,48]{2,1,0:T(2,128)(2,1)} reshape(bf16[4,2,49152]{2,1,0:T(2,128)(2,1)} %all-to-all-done) | data formatting | bytes 1572864
  128.8 8.1 %copy.23 = bf16[1,48,8192]{2,1,0:T(8,128)(2,1)S(1)} copy(bf16[1,48,8192]{1,0,2:T(2,128)(2,1)} %bitcast.78) | data formatting | bytes 1572864 | tf_op jit(solution)/shard_map/all_to_all | solution.py:67
  138.9 6.9 %multiply_reduce_fusion.1 = (f32[128]{0:T(128)S(1)}, f32[128,2048]{1,0:T(8,128)S(1)}) fusion(bf16[3200,2048]{1,0:T(8,128)(2,1)} %all-gather.3.cloned.1.call-done, bf16[1,128,3200]{2,1,0:T(8,128)(2,1)S(1)} %all-gather), kind=kOutput, calls=%fused_computation.31 | convolution fusion | flops 1678770048 | bytes 14975488 | tf_op jit(solution)/shard_map/dot_general | solution.py:45
  145.8 11.2 %psum.28 = f32[128]{0:T(128)S(1)} all-reduce(f32[128]{0:T(128)S(1)} %get-tuple-element.24), channel_id=1, replica_groups=mesh['dp'=8,'seq'=4] {'seq'}, use_global_device_ids=true, to_apply=%region_3.4 | all-reduce | flops 128 | bytes 1024 | tf_op jit(solution)/shard_map/psum | solution.py:72
  157.4 16.4 %all-reduce = (f32[128]{0:T(128)S(1)}, f32[8192]{0:T(1024)S(1)}) all-reduce(f32[128]{0:T(128)S(1)} %get-tuple-element.13, f32[8192]{0:T(1024)S(1)} %add_dynamic-update-slice_fusion), channel_id=1, replica_groups=mesh['dp'=8,'seq'=4] {'seq'}, use_global_device_ids=true, to_apply=%region_5.6 | all-reduce | flops 8320 | bytes 66560 | tf_op jit(solution)/shard_map/psum | solution.py:72
  173.9 5.1 %multiply_reduce_fusion = (f32[3200]{0:T(1024)S(1)}, f32[2048,3200]{1,0:T(8,128)S(1)}) fusion(bf16[1,128,3200]{2,1,0:T(8,128)(2,1)S(1)} %all-gather, f32[128,2048]{1,0:T(8,128)} %copy-done.2, f32[128]{0:T(128)S(1)} %multiply_multiply_fusion, f32[128]{0:T(128)S(1)} %add_rsqrt_fusion.1, f32[2048]{0:T(1024)S(1)} %dynamic_slice.14, ...), kind=kOutput, calls=%fused_computation.12 | convolution fusion | flops 1692922752 | bytes 28628608 | tf_op jit(solution)/shard_map/dot_general | solution.py:93
  179.1 22.1 %fusion.6 = bf16[3200,2048]{0,1:T(8,128)(2,1)} fusion(f32[2048,3200]{1,0:T(8,128)S(1)} %get-tuple-element.27, f32[3200]{0:T(1024)S(1)} %convert_reduce_fusion, f32[2048]{0:T(1024)S(1)} %bitcast.80, f32[3200]{0:T(1024)S(1)} %reduce.2, f32[3200]{0:T(1024)S(1)} %add_sqrt_fusion), kind=kLoop, calls=%fused_computation.13 | loop fusion | flops 117964800 | bytes 39368192 | tf_op jit(solution)/shard_map/convert_element_type | solution.py:97
  201.2 18.3 %copy.26 = bf16[3200,2048]{1,0:T(8,128)(2,1)} copy(bf16[3200,2048]{0,1:T(8,128)(2,1)} %fusion.6) | data formatting | bytes 26214400
  219.5 22.3 %psum.31 = f32[8192]{0:T(1024)S(1)} all-reduce(f32[8192]{0:T(1024)S(1)} %get-tuple-element.15), channel_id=1, replica_groups=mesh['dp'=8,'seq'=4] {'dp'}, use_global_device_ids=true, to_apply=%region_13.14 | all-reduce | flops 8192 | bytes 65536 | tf_op jit(solution)/shard_map/psum | solution.py:102
  242.5 71.1 %reduce-scatter.4.cloned.1.call-done = bf16[400,2048]{1,0:T(8,128)(2,1)} async-done(((bf16[3200,2048]{1,0:T(8,128)(2,1)}), bf16[400,2048]{1,0:T(8,128)(2,1)}) %reduce-scatter.4.cloned.1.call-update) | async-done | bytes 1638416
  313.6 2.8 copy.27
  316.4 2.5 convert_multiply_fusion.2
  318.9 5.2 %copy.25 = f32[400,2048]{1,0:T(8,128)} copy(f32[400,2048]{0,1:T(8,128)} %convert_multiply_fusion.2) | data formatting | bytes 6553600
  (53 shorter events, 10.8 us)
Async XLA Ops:
  7.2 79.3 %copy-start = (s32[1,128]{1,0:T(1,128)S(1)}, s32[1,128]{1,0:T(1,128)}, u32[]{:S(2)}) copy-start(s32[1,128]{1,0:T(1,128)} %param.14) | copy-start | bytes 1540
  7.2 82.8 %copy-start.5 = (s32[1,1,3200]{2,1,0:T(1,128)S(1)}, s32[1,1,3200]{2,1,0:T(1,128)}, u32[]{:S(2)}) copy-start(s32[1,1,3200]{2,1,0:T(1,128)} %param.15) | copy-start | bytes 38404
  7.2 83.6 %copy-start.6 = (f32[1,1,3200]{2,1,0:T(1,128)S(1)}, f32[1,1,3200]{2,1,0:T(1,128)}, u32[]{:S(2)}) copy-start(f32[1,1,3200]{2,1,0:T(1,128)} %param.16) | copy-start | bytes 38404
  7.2 131.7 %all-gather.3.cloned.1.call-start = ((), (), s32[]{:S(2)}) async-start(), calls=%async_computation.2 | async-start | bytes 14745600 | tf_op jit(solution)/shard_map/all_gather | solution.py:47
  13.0 80.0 %copy-start.4 = (bf16[1,32,3200]{2,1,0:T(8,128)(2,1)S(1)}, bf16[1,32,3200]{2,1,0:T(8,128)(2,1)}, u32[]{:S(2)}) copy-start(bf16[1,32,3200]{2,1,0:T(8,128)(2,1)} %param.9) | copy-start | bytes 614404
  13.0 107.5 %copy-start.1 = (bf16[1,128,8192]{2,1,0:T(8,128)(2,1)S(1)}, bf16[1,128,8192]{2,1,0:T(8,128)(2,1)}, u32[]{:S(2)}) copy-start(bf16[1,128,8192]{2,1,0:T(8,128)(2,1)} %param.12) | copy-start | bytes 6291460
  80.0 42.9 %all-to-all-start = ((bf16[4,2,49152]{2,1,0:T(2,128)(2,1)}), bf16[4,2,49152]{2,1,0:T(2,128)(2,1)}, u32[]{:S(2)}, u32[]{:S(2)}) async-start(bf16[4,2,49152]{2,1,0:T(2,128)(2,1)} %reshape.423), calls=%async_computation | async-start | bytes 1572864 | tf_op jit(solution)/shard_map/all_to_all | solution.py:67
  86.5 227.1 %reduce-scatter.4.cloned.1.call-start = ((), (), s32[]{:S(2)}) async-start(), calls=%async_computation.3 | async-start | bytes 14745600
  138.9 35.0 %copy-start.3 = (bf16[128,2048]{1,0:T(8,128)(2,1)}, bf16[128,2048]{1,0:T(8,128)(2,1)S(1)}, u32[]{:S(2)}) copy-start(bf16[128,2048]{1,0:T(8,128)(2,1)S(1)} %gather_fusion.2) | copy-start | bytes 1572868
  145.8 28.1 %copy-start.2 = (f32[128,2048]{1,0:T(8,128)}, f32[128,2048]{1,0:T(8,128)S(1)}, u32[]{:S(2)}) copy-start(f32[128,2048]{1,0:T(8,128)S(1)} %get-tuple-element.25) | copy-start | bytes 3145732
  173.9 5.2 %copy-start.7 = (f32[1,2048]{1,0:T(1,128)S(1)}, f32[1,2048]{1,0:T(1,128)}, u32[]{:S(2)}) copy-start(f32[1,2048]{1,0:T(1,128)} %param.17) | copy-start | bytes 24580
Sparse Core Ops, SparseCore 0:
  9.9 76.9 all-gather.2
  219.7 93.9 reduce-scatter.3
